TPU v7x, 512 devices: a whole 4x4x16 slice. The times are simulated.
512 devices in a mesh: spec: 64 (over x_hi, z, core), img: 8 (over x_lo, y).
Axes of the slice: x: 4 (x_hi: 2, x_lo: 2; x = x_hi * 2 + x_lo), y: 4, z: 16, core: 2. Of those that a mesh axis runs over, the one named last changes fastest.
Arguments:
- spec_emb: bfloat16 [8192, 1024], P('spec', 'img'), may hold values from -1024 to 1024
- img_emb: bfloat16 [2048, 1024], P('img', 'spec'), may hold values from -16 to 16
- grad_spec: bfloat16 [8192, 1024], P('spec', 'img'), may hold values from -6 to 6
- grad_img: bfloat16 [2048, 1024], P('img', 'spec'), may hold values from -6 to 6
Outputs:
- spec_emb_grad: bfloat16 [8192, 1024], P('spec', 'img')
- img_emb_grad: bfloat16 [2048, 1024], P('img', 'spec')
All inputs are finite; a program needn't handle non-finite values.
Results may differ from a plain program's by a relative error of at most 0.0109.
Values may be sent and summed in bfloat16 or wider, within the bound.
No kernel may reach another device: no remote copies, remote signals or barrier semaphores. Data moves between devices by JAX's collectives and lax.ppermute only.
A program may use at most 64 MiB of HBM per device.

v0:
```python
import jax
import jax.numpy as jnp
from jax import lax
from jax.sharding import Mesh
from jax.sharding import PartitionSpec as P

D = 1024
HEADS = 16
SPEC = ("spec_0", "spec_1", "spec_2")


def collected_together(value, axis):
    leaves = jax.tree.leaves(value)
    order = sorted(range(len(leaves)), key=lambda k: -leaves[k].size)
    width = (1, *leaves[order[0]].shape)[-1]
    lines = [
        jnp.pad(leaves[k].reshape(-1), (0, -leaves[k].size % width)).reshape(-1, width)
        for k in order
    ]
    both, at, found = (lax.all_gather(jnp.concatenate(lines), axis), 0, {})
    for k, line in zip(order, lines):
        piece = both[:, at : at + len(line)].reshape(len(both), -1)
        found[k] = piece[:, : leaves[k].size].reshape(-1, *leaves[k].shape)
        at += len(line)
    numbers = iter(range(len(leaves)))
    return jax.tree.map(lambda _: found[next(numbers)], value)


def combined_by_axis(value, axes, combine):
    for axis in axes:
        pieces = collected_together(value, axis)
        value = jax.tree.map(lambda part: part[0], pieces)
        for k in range(1, lax.axis_size(axis)):
            value = combine(value, jax.tree.map(lambda part: part[k], pieces))
    return value


def turned_gather(arrays, axis, dims):
    turned = [jnp.moveaxis(a, dim, 0) for a, dim in zip(arrays, dims)]
    both = jnp.concatenate([t.reshape(len(t), -1) for t in turned], axis=1)
    whole, at, done = (lax.all_gather(both, axis, axis=0, tiled=True), 0, [])
    for t, dim in zip(turned, dims):
        piece = whole[:, at : at + t[0].size].reshape(-1, *t.shape[1:])
        done.append(jnp.moveaxis(piece, 0, dim))
        at += t[0].size
    return tuple(done)


def in_blocks(value, dim, peers):
    before, after = (value.shape[:dim], value.shape[dim + 1 :])
    return jnp.moveaxis(value.reshape(*before, peers, -1, *after), dim, 0)


def summed_on_arrival(value, axis, dim):
    peers = lax.axis_size(axis)
    pieces = lax.all_to_all(in_blocks(value, dim, peers), axis, 0, 0, tiled=True)
    return jnp.sum(pieces, axis=0)


def pair_combine(left_part, right_part):
    highest = jnp.maximum(left_part[0], right_part[0])
    left_factor = jnp.exp(left_part[0] - highest)
    right_factor = jnp.exp(right_part[0] - highest)
    return (
        highest,
        left_part[1] * left_factor + right_part[1] * right_factor,
        left_part[2] * left_factor + right_part[2] * right_factor,
    )


def local_moments(scores, moment, dim):
    highest = jnp.max(scores, axis=dim, keepdims=True)
    scaled = jnp.exp(scores - highest)
    return (
        highest,
        jnp.sum(scaled, axis=dim, keepdims=True),
        jnp.sum(scaled * moment, axis=dim, keepdims=True),
    )


def column_totals(scores, moment):
    highest, total, weighted = combined_by_axis(
        local_moments(scores, moment, 1), SPEC, pair_combine
    )
    weights = jnp.exp(scores - highest) / total
    delta = weighted / total
    return (weights, delta)


def local_row_totals(scores, moment):
    scaled = jnp.exp(scores - jnp.max(scores, axis=2, keepdims=True))
    weights = scaled / jnp.sum(scaled, axis=2, keepdims=True)
    return (weights, jnp.sum(weights * moment, axis=2, keepdims=True))


def score_block(spec_rows, spec_grad, image_rows, image_grad, row_rule, column_rule):
    scale = (D // HEADS) ** (-0.5)
    scores = (
        jnp.einsum("shd,ihd->hsi", spec_rows, image_rows, preferred_element_type=jnp.float32)
        * scale
    )
    row_moment = jnp.einsum(
        "shd,ihd->hsi", spec_grad, image_rows, preferred_element_type=jnp.float32
    )
    column_moment = jnp.einsum(
        "shd,ihd->hsi", spec_rows, image_grad, preferred_element_type=jnp.float32
    )
    row_weight, row_delta = row_rule(scores, row_moment)
    column_weight, column_delta = column_rule(scores, column_moment)
    slope = (
        row_weight * (row_moment - row_delta) + column_weight * (column_moment - column_delta)
    ).astype(jnp.bfloat16)
    spec_part = scale * jnp.einsum(
        "hsi,ihd->shd", slope, image_rows, preferred_element_type=jnp.float32
    )
    spec_part = spec_part + jnp.einsum(
        "hsi,ihd->shd",
        column_weight.astype(jnp.bfloat16),
        image_grad,
        preferred_element_type=jnp.float32,
    )
    image_part = scale * jnp.einsum(
        "hsi,shd->ihd", slope, spec_rows, preferred_element_type=jnp.float32
    )
    image_part = image_part + jnp.einsum(
        "hsi,shd->ihd",
        row_weight.astype(jnp.bfloat16),
        spec_grad,
        preferred_element_type=jnp.float32,
    )
    return (spec_part, image_part)


def shards(spec_emb, img_emb, grad_spec, grad_img):
    head_size = D // HEADS
    spec_count = spec_emb.shape[0]
    image_all, image_grad_all = turned_gather((img_emb, grad_img), SPEC, (1, 1))
    image_local, image_grad_local = (
        lax.all_to_all(image_all, "img", split_axis=1, concat_axis=0, tiled=True),
        lax.all_to_all(image_grad_all, "img", split_axis=1, concat_axis=0, tiled=True),
    )
    local_width = spec_emb.shape[1]
    local_heads = local_width // head_size
    image_count = image_local.shape[0]
    spec_heads = spec_emb.reshape(spec_count, local_heads, head_size)
    spec_grad_heads = grad_spec.reshape(spec_count, local_heads, head_size)
    image_heads = image_local.reshape(image_count, local_heads, head_size)
    image_grad_heads = image_grad_local.reshape(image_count, local_heads, head_size)
    spec_parts = []
    image_parts = []
    for head_index in range(local_heads):
        window = slice(head_index, head_index + 1)
        spec_part, image_part = score_block(
            spec_heads[:, window],
            spec_grad_heads[:, window],
            image_heads[:, window],
            image_grad_heads[:, window],
            local_row_totals,
            column_totals,
        )
        spec_parts.append(spec_part)
        image_parts.append(image_part)
    spec_result = (
        jnp.concatenate(spec_parts, axis=1).reshape(spec_count, local_width).astype(jnp.bfloat16)
    )
    image_total = jnp.concatenate(image_parts, axis=1).reshape(image_count, local_width)
    image_back = lax.all_to_all(image_total, "img", split_axis=0, concat_axis=1, tiled=True)
    image_result = summed_on_arrival(image_back, SPEC, 1).astype(jnp.bfloat16)
    return (spec_result, image_result)


def solution(mesh):
    split = Mesh(
        mesh.devices.reshape(2, 16, 2, mesh.shape["img"]), ("spec_0", "spec_1", "spec_2", "img")
    )
    return jax.shard_map(
        shards,
        mesh=split,
        in_specs=(P(SPEC, "img"), P("img", SPEC), P(SPEC, "img"), P("img", SPEC)),
        out_specs=(P(SPEC, "img"), P("img", SPEC)),
        check_vma=False,
    )
```

profile of v0, /device:TPU:33, one launch (start us, length us, event | category | flops | bytes accessed | tf_op | source)
XLA Modules:
  0.0 371.6 jit_solution(16061481993177456034)
XLA Ops:
  7.2 1.3 pad_maximum_fusion.2
  8.6 148.4 %all-gather.14.cloned.1.call-done = bf16[1024,512]{1,0:T(8,128)(2,1)} async-done(((bf16[16,512]{1,0:T(8,128)(2,1)}), bf16[1024,512]{1,0:T(8,128)(2,1)}) %all-gather.14.cloned.1.call-update) | async-done | bytes 1048592 | tf_op jit(solution)/shard_map/all_gather | solution.py:41
  157.0 2.3 fusion.160
  159.3 4.1 %all-to-all-start = ((bf16[256,8,128]{0,2,1:T(8,128)(2,1)}), bf16[256,8,128]{0,2,1:T(8,128)(2,1)S(1)}, u32[]{:S(2)}, u32[]{:S(2)}) async-start(bf16[256,8,128]{0,2,1:T(8,128)(2,1)} %bitcast.3), calls=%async_computation | async-start | bytes 1048576 | tf_op jit(solution)/shard_map/all_to_all | solution.py:139
  163.6 0.6 copy-done.6
  164.3 7.4 %all-to-all-done = bf16[256,8,128]{0,2,1:T(8,128)(2,1)S(1)} async-done(((bf16[256,8,128]{0,2,1:T(8,128)(2,1)}), bf16[256,8,128]{0,2,1:T(8,128)(2,1)S(1)}, u32[]{:S(2)}, u32[]{:S(2)}) %all-to-all-start) | async-done | bytes 524320 | tf_op jit(solution)/shard_map/all_to_all | solution.py:139
  171.7 4.7 %all-to-all-start.1 = ((bf16[256,8,128]{0,2,1:T(8,128)(2,1)}), bf16[256,8,128]{0,2,1:T(8,128)(2,1)S(1)}, u32[]{:S(2)}, u32[]{:S(2)}) async-start(bf16[256,8,128]{0,2,1:T(8,128)(2,1)} %bitcast.15), calls=%async_computation.1 | async-start | bytes 1048576 | tf_op jit(solution)/shard_map/all_to_all | solution.py:140
  177.0 0.6 fusion.157
  177.6 0.6 fusion.156
  178.2 6.3 %all-to-all-done.1 = bf16[256,8,128]{0,2,1:T(8,128)(2,1)S(1)} async-done(((bf16[256,8,128]{0,2,1:T(8,128)(2,1)}), bf16[256,8,128]{0,2,1:T(8,128)(2,1)S(1)}, u32[]{:S(2)}, u32[]{:S(2)}) %all-to-all-start.1) | async-done | bytes 524320 | tf_op jit(solution)/shard_map/all_to_all | solution.py:140
  184.5 1.1 copy.24
  185.6 1.3 reshape.521
  186.9 1.1 fusion.12
  188.0 4.9 %all-gather.6 = f32[2,3,2048]{2,1,0:T(4,128)S(1)} all-gather(f32[1,3,2048]{2,1,0:T(4,128)S(1)} %maximum_bitcast_fusion), channel_id=2, replica_groups=mesh['spec_0'=2,'spec_1'=16,'spec_2'=2,'img'=8] {'spec_0'}, dimensions={0}, use_global_device_ids=true | all-gather | bytes 73728 | tf_op jit(solution)/shard_map/all_gather | solution.py:20
  193.0 22.7 %all-gather.7 = f32[16,3,2048]{2,1,0:T(4,128)S(1)} all-gather(f32[1,3,2048]{2,1,0:T(4,128)S(1)} %maximum_bitcast_fusion.1), channel_id=3, replica_groups=mesh['spec_0'=2,'spec_1'=16,'spec_2'=2,'img'=8] {'spec_1'}, dimensions={0}, use_global_device_ids=true | all-gather | bytes 417792 | tf_op jit(solution)/shard_map/all_gather | solution.py:20
  216.5 12.0 %all-gather.8 = f32[2,3,2048]{2,1,0:T(4,128)S(1)} all-gather(f32[1,3,2048]{2,1,0:T(4,128)S(1)} %maximum_bitcast_fusion.2), channel_id=4, replica_groups=mesh['spec_0'=2,'spec_1'=16,'spec_2'=2,'img'=8] {'spec_2'}, dimensions={0}, use_global_device_ids=true | all-gather | bytes 73728 | tf_op jit(solution)/shard_map/all_gather | solution.py:20
  229.1 1.5 fusion.8
  231.2 0.7 copy-done.3
  231.9 1.1 fusion.15
  233.0 4.9 %all-gather.9 = f32[2,3,2048]{2,1,0:T(4,128)S(1)} all-gather(f32[1,3,2048]{2,1,0:T(4,128)S(1)} %maximum_bitcast_fusion.3), channel_id=5, replica_groups=mesh['spec_0'=2,'spec_1'=16,'spec_2'=2,'img'=8] {'spec_0'}, dimensions={0}, use_global_device_ids=true | all-gather | bytes 73728 | tf_op jit(solution)/shard_map/all_gather | solution.py:20
  238.1 23.8 %all-gather.10 = f32[16,3,2048]{2,1,0:T(4,128)S(1)} all-gather(f32[1,3,2048]{2,1,0:T(4,128)S(1)} %maximum_bitcast_fusion.4), channel_id=6, replica_groups=mesh['spec_0'=2,'spec_1'=16,'spec_2'=2,'img'=8] {'spec_1'}, dimensions={0}, use_global_device_ids=true | all-gather | bytes 417792 | tf_op jit(solution)/shard_map/all_gather | solution.py:20
  262.7 9.8 %all-gather.11 = f32[2,3,2048]{2,1,0:T(4,128)S(1)} all-gather(f32[1,3,2048]{2,1,0:T(4,128)S(1)} %maximum_bitcast_fusion.5), channel_id=7, replica_groups=mesh['spec_0'=2,'spec_1'=16,'spec_2'=2,'img'=8] {'spec_2'}, dimensions={0}, use_global_device_ids=true | all-gather | bytes 73728 | tf_op jit(solution)/shard_map/all_gather | solution.py:20
  273.0 1.5 fusion.6
  276.4 17.6 %all_to_all.53 = f32[8,256,128]{1,2,0:T(8,128)} all-to-all(f32[8,256,128]{1,2,0:T(8,128)S(1)} %copy.29), channel_id=1, replica_groups=mesh['spec_0'=2,'spec_1'=16,'spec_2'=2,'img'=8] {'img'}, dimensions={0} | all-to-all | bytes 2097152 | tf_op jit(solution)/shard_map/all_to_all | solution.py:167
  294.0 13.2 %all-to-all-start.3 = ((f32[64,256,16]{1,2,0:T(8,128)}), f32[64,256,16]{1,2,0:T(8,128)}, u32[]{:S(2)}, u32[]{:S(2)}) async-start(f32[64,256,16]{1,2,0:T(8,128)} %bitcast.185), calls=%async_computation.3 | async-start | bytes 2097152 | tf_op jit(solution)/shard_map/all_to_all | solution.py:56
  307.4 0.8 copy-done.1
  308.4 0.8 copy-done.4
  309.2 0.8 fusion.5
  310.0 0.8 fusion.4
  310.8 0.7 copy.30
  311.5 51.3 %all-to-all-done.3 = f32[64,256,16]{1,2,0:T(8,128)} async-done(((f32[64,256,16]{1,2,0:T(8,128)}), f32[64,256,16]{1,2,0:T(8,128)}, u32[]{:S(2)}, u32[]{:S(2)}) %all-to-all-start.3) | async-done | bytes 1048608 | tf_op jit(solution)/shard_map/all_to_all | solution.py:56
  362.8 1.9 reduce_sum.101
  (44 shorter events, 6.7 us)
Async XLA Ops:
  7.2 149.8 %all-gather.14.cloned.1.call-start = ((), (), s32[]{:S(2)}) async-start(), calls=%async_computation.4 | async-start | bytes 1064960 | tf_op jit(solution)/shard_map/all_gather | solution.py:41
  159.3 4.2 %copy-start.5 = (bf16[128,128]{1,0:T(8,128)(2,1)S(1)}, bf16[128,128]{1,0:T(8,128)(2,1)}, u32[]{:S(2)}) copy-start(bf16[128,128]{1,0:T(8,128)(2,1)} %param.4) | copy-start | bytes 98308
  159.3 12.4 %all-to-all-start = ((bf16[256,8,128]{0,2,1:T(8,128)(2,1)}), bf16[256,8,128]{0,2,1:T(8,128)(2,1)S(1)}, u32[]{:S(2)}, u32[]{:S(2)}) async-start(bf16[256,8,128]{0,2,1:T(8,128)(2,1)} %bitcast.3), calls=%async_computation | async-start | bytes 1048576 | tf_op jit(solution)/shard_map/all_to_all | solution.py:139
  163.4 0.8 copy-start.6
  171.7 12.7 %all-to-all-start.1 = ((bf16[256,8,128]{0,2,1:T(8,128)(2,1)}), bf16[256,8,128]{0,2,1:T(8,128)(2,1)S(1)}, u32[]{:S(2)}, u32[]{:S(2)}) async-start(bf16[256,8,128]{0,2,1:T(8,128)(2,1)} %bitcast.15), calls=%async_computation.1 | async-start | bytes 1048576 | tf_op jit(solution)/shard_map/all_to_all | solution.py:140
  186.9 1.1 copy-start.2
  230.9 1.0 copy-start.3
  274.5 0.8 copy-start
  294.0 68.8 %all-to-all-start.3 = ((f32[64,256,16]{1,2,0:T(8,128)}), f32[64,256,16]{1,2,0:T(8,128)}, u32[]{:S(2)}, u32[]{:S(2)}) async-start(f32[64,256,16]{1,2,0:T(8,128)} %bitcast.185), calls=%async_computation.3 | async-start | bytes 2097152 | tf_op jit(solution)/shard_map/all_to_all | solution.py:56
  307.1 1.0 copy-start.1
  308.2 1.0 copy-start.4
Sparse Core Ops, SparseCore 0:
  11.8 145.1 all-gather.13
where the time goes:
time: 372 us
  waiting for transfers between devices  214 us (58%)
  blocking collectives  95.7 us (26%)
  starting transfers between devices  22.1 us (6%)
  between operations  14.3 us (4%)
  local copies, waits for them, and re-layouts  10.3 us (3%)
  other arithmetic  8.32 us (2%)
  matrix products  7.43 us (2%)
    all_gather x1, waiting for transfers between devices, turned_gather(): whole, at, done = (lax.all_gather(both, axis, axis=0, tiled=True), 0, [])  148 us
    all_gather x6, blocking collectives, collected_together(): both, at, found = (lax.all_gather(jnp.concatenate(lines), axis), 0, {})  78.1 us
    all_to_all x1, waiting for transfers between devices, summed_on_arrival(): lax.all_to_all(in_blocks(value, dim, peers), axis, 0, 0, tiled=True)  51.3 us
    all_to_all x1, blocking collectives, shards(): lax.all_to_all(image_total, 'img', split_axis=0, concat_axis=1, tiled=True)  17.6 us
    all_to_all x1, starting transfers between devices, summed_on_arrival(): lax.all_to_all(in_blocks(value, dim, peers), axis, 0, 0, tiled=True)  13.2 us
  transfers between devices with their start and end apart: 4, of which 4 were waited for; matrix products, arithmetic and copies ran while one was open for 1% of the time, Pallas kernels for 0%

commit v1 on v0

--- a/solution.py
+++ b/solution.py
@@ -38,7 +38,13 @@
 def turned_gather(arrays, axis, dims):
     turned = [jnp.moveaxis(a, dim, 0) for a, dim in zip(arrays, dims)]
     both = jnp.concatenate([t.reshape(len(t), -1) for t in turned], axis=1)
-    whole, at, done = (lax.all_gather(both, axis, axis=0, tiled=True), 0, [])
+    whole, at, done = (
+        jnp.concatenate(
+            lax.all_to_all(jnp.stack([both] * lax.axis_size(axis)), axis, 0, 0), axis=0
+        ),
+        0,
+        [],
+    )
     for t, dim in zip(turned, dims):
         piece = whole[:, at : at + t[0].size].reshape(-1, *t.shape[1:])
         done.append(jnp.moveaxis(piece, 0, dim))

time: 372 us -> 279 us (0.75)
  waiting for transfers between devices: 214 us -> 64.2 us
  blocking collectives: 95.7 us -> 170 us
  between operations: 14.3 us -> 0.9 us
    all_gather x1 -> x0, waiting for transfers between devices: 148 us -> none  [turned_gather(): whole, at, done = (lax.all_gather(both, axis, axis=0, tiled=True), 0, [])]
    all_to_all x0 -> x1, blocking collectives: none -> 74 us  [turned_gather(): lax.all_to_all(jnp.stack([both] * lax.axis_size(axis)), axis, 0, 0)]
  transfers between devices with their start and end apart: 4 -> 3, of which waited for: 4 -> 3; matrix products, arithmetic and copies ran while one was open for 1% -> 2% of each run, Pallas kernels for 0% -> 0%
where the time goes in v1:
time: 279 us; the launch traced here: 278 us
  blocking collectives  170 us (61%)
  waiting for transfers between devices  64.2 us (23%)
  starting transfers between devices  18.7 us (7%)
  local copies, waits for them, and re-layouts  9.16 us (3%)
  other arithmetic  7.71 us (3%)
  matrix products  7.43 us (3%)
    all_gather x6, blocking collectives, collected_together(): both, at, found = (lax.all_gather(jnp.concatenate(lines), axis), 0, {})  78.1 us
    all_to_all x1, blocking collectives, turned_gather(): lax.all_to_all(jnp.stack([both] * lax.axis_size(axis)), axis, 0, 0)  74 us
    all_to_all x1, waiting for transfers between devices, summed_on_arrival(): lax.all_to_all(in_blocks(value, dim, peers), axis, 0, 0, tiled=True)  51.3 us
    all_to_all x1, blocking collectives, shards(): lax.all_to_all(image_total, 'img', split_axis=0, concat_axis=1, tiled=True)  17.6 us
    all_to_all x1, starting transfers between devices, summed_on_arrival(): lax.all_to_all(in_blocks(value, dim, peers), axis, 0, 0, tiled=True)  10.9 us
    all_to_all x1, waiting for transfers between devices, shards(): lax.all_to_all(image_grad_all, 'img', split_axis=1, concat_axis=0, tiled=...  6.61 us
    all_to_all x1, waiting for transfers between devices, shards(): lax.all_to_all(image_all, 'img', split_axis=1, concat_axis=0, tiled=True)  6.3 us
  transfers between devices with their start and end apart: 3, of which 3 were waited for; matrix products, arithmetic and copies ran while one was open for 2% of the time, Pallas kernels for 0%

profile of v1, /device:TPU:33, one launch (start us, length us, event | category | flops | bytes accessed | tf_op | source)
XLA Modules:
  0.0 277.9 jit_solution(12040828502538205042)
XLA Ops:
  0.6 0.7 pad_maximum_fusion.2
  1.5 74.0 %all_to_all.58 = bf16[64,16,512]{2,1,0:T(8,128)(2,1)S(1)} all-to-all(bf16[64,16,512]{2,1,0:T(8,128)(2,1)S(1)} %stack.2), channel_id=1, replica_groups=mesh['spec_0'=2,'spec_1'=16,'spec_2'=2,'img'=8] {'spec_0','spec_1','spec..., dimensions={0} | all-to-all | bytes 2097152 | tf_op jit(solution)/shard_map/all_to_all | solution.py:43
  75.5 1.1 fusion.160
  76.6 4.4 %all-to-all-start.1 = ((bf16[256,8,128]{0,2,1:T(8,128)(2,1)}), bf16[256,8,128]{0,2,1:T(8,128)(2,1)S(1)}, u32[]{:S(2)}, u32[]{:S(2)}) async-start(bf16[256,8,128]{0,2,1:T(8,128)(2,1)} %bitcast.4), calls=%async_computation.1 | async-start | bytes 1048576 | tf_op jit(solution)/shard_map/all_to_all | solution.py:145
  81.0 0.6 copy-done.6
  81.8 6.3 %all-to-all-done.1 = bf16[256,8,128]{0,2,1:T(8,128)(2,1)S(1)} async-done(((bf16[256,8,128]{0,2,1:T(8,128)(2,1)}), bf16[256,8,128]{0,2,1:T(8,128)(2,1)S(1)}, u32[]{:S(2)}, u32[]{:S(2)}) %all-to-all-start.1) | async-done | bytes 524320 | tf_op jit(solution)/shard_map/all_to_all | solution.py:145
  88.1 3.5 %all-to-all-start.2 = ((bf16[256,8,128]{0,2,1:T(8,128)(2,1)}), bf16[256,8,128]{0,2,1:T(8,128)(2,1)S(1)}, u32[]{:S(2)}, u32[]{:S(2)}) async-start(bf16[256,8,128]{0,2,1:T(8,128)(2,1)} %bitcast.16), calls=%async_computation.2 | async-start | bytes 1048576 | tf_op jit(solution)/shard_map/all_to_all | solution.py:146
  92.1 0.6 fusion.157
  92.7 0.6 fusion.156
  93.3 6.6 %all-to-all-done.2 = bf16[256,8,128]{0,2,1:T(8,128)(2,1)S(1)} async-done(((bf16[256,8,128]{0,2,1:T(8,128)(2,1)}), bf16[256,8,128]{0,2,1:T(8,128)(2,1)S(1)}, u32[]{:S(2)}, u32[]{:S(2)}) %all-to-all-start.2) | async-done | bytes 524320 | tf_op jit(solution)/shard_map/all_to_all | solution.py:146
  99.9 1.1 copy.32
  101.0 1.3 reshape.527
  102.3 1.1 fusion.12
  103.4 4.9 %all-gather.6 = f32[2,3,2048]{2,1,0:T(4,128)S(1)} all-gather(f32[1,3,2048]{2,1,0:T(4,128)S(1)} %maximum_bitcast_fusion), channel_id=2, replica_groups=mesh['spec_0'=2,'spec_1'=16,'spec_2'=2,'img'=8] {'spec_0'}, dimensions={0}, use_global_device_ids=true | all-gather | bytes 73728 | tf_op jit(solution)/shard_map/all_gather | solution.py:20
  108.5 23.2 %all-gather.7 = f32[16,3,2048]{2,1,0:T(4,128)S(1)} all-gather(f32[1,3,2048]{2,1,0:T(4,128)S(1)} %maximum_bitcast_fusion.1), channel_id=3, replica_groups=mesh['spec_0'=2,'spec_1'=16,'spec_2'=2,'img'=8] {'spec_1'}, dimensions={0}, use_global_device_ids=true | all-gather | bytes 417792 | tf_op jit(solution)/shard_map/all_gather | solution.py:20
  132.5 12.5 %all-gather.8 = f32[2,3,2048]{2,1,0:T(4,128)S(1)} all-gather(f32[1,3,2048]{2,1,0:T(4,128)S(1)} %maximum_bitcast_fusion.2), channel_id=4, replica_groups=mesh['spec_0'=2,'spec_1'=16,'spec_2'=2,'img'=8] {'spec_2'}, dimensions={0}, use_global_device_ids=true | all-gather | bytes 73728 | tf_op jit(solution)/shard_map/all_gather | solution.py:20
  145.5 1.5 fusion.8
  147.7 0.7 copy-done.3
  148.4 1.1 fusion.15
  149.4 4.9 %all-gather.9 = f32[2,3,2048]{2,1,0:T(4,128)S(1)} all-gather(f32[1,3,2048]{2,1,0:T(4,128)S(1)} %maximum_bitcast_fusion.3), channel_id=5, replica_groups=mesh['spec_0'=2,'spec_1'=16,'spec_2'=2,'img'=8] {'spec_0'}, dimensions={0}, use_global_device_ids=true | all-gather | bytes 73728 | tf_op jit(solution)/shard_map/all_gather | solution.py:20
  154.5 22.8 %all-gather.10 = f32[16,3,2048]{2,1,0:T(4,128)S(1)} all-gather(f32[1,3,2048]{2,1,0:T(4,128)S(1)} %maximum_bitcast_fusion.4), channel_id=6, replica_groups=mesh['spec_0'=2,'spec_1'=16,'spec_2'=2,'img'=8] {'spec_1'}, dimensions={0}, use_global_device_ids=true | all-gather | bytes 417792 | tf_op jit(solution)/shard_map/all_gather | solution.py:20
  178.1 9.8 %all-gather.11 = f32[2,3,2048]{2,1,0:T(4,128)S(1)} all-gather(f32[1,3,2048]{2,1,0:T(4,128)S(1)} %maximum_bitcast_fusion.5), channel_id=7, replica_groups=mesh['spec_0'=2,'spec_1'=16,'spec_2'=2,'img'=8] {'spec_2'}, dimensions={0}, use_global_device_ids=true | all-gather | bytes 73728 | tf_op jit(solution)/shard_map/all_gather | solution.py:20
  188.4 1.5 fusion.6
  191.8 17.6 %all_to_all.59 = f32[8,256,128]{1,2,0:T(8,128)} all-to-all(f32[8,256,128]{1,2,0:T(8,128)S(1)} %copy.37), channel_id=1, replica_groups=mesh['spec_0'=2,'spec_1'=16,'spec_2'=2,'img'=8] {'img'}, dimensions={0} | all-to-all | bytes 2097152 | tf_op jit(solution)/shard_map/all_to_all | solution.py:173
  209.4 10.9 %all-to-all-start.4 = ((f32[64,256,16]{1,2,0:T(8,128)}), f32[64,256,16]{1,2,0:T(8,128)}, u32[]{:S(2)}, u32[]{:S(2)}) async-start(f32[64,256,16]{1,2,0:T(8,128)} %bitcast.186), calls=%async_computation.4 | async-start | bytes 2097152 | tf_op jit(solution)/shard_map/all_to_all | solution.py:62
  220.6 0.8 copy-done.1
  221.6 0.8 copy-done.4
  222.4 0.8 fusion.5
  223.2 0.8 fusion.4
  223.9 0.7 copy.38
  224.7 51.3 %all-to-all-done.4 = f32[64,256,16]{1,2,0:T(8,128)} async-done(((f32[64,256,16]{1,2,0:T(8,128)}), f32[64,256,16]{1,2,0:T(8,128)}, u32[]{:S(2)}, u32[]{:S(2)}) %all-to-all-start.4) | async-done | bytes 1048608 | tf_op jit(solution)/shard_map/all_to_all | solution.py:62
  276.0 1.9 reduce_sum.101
  (43 shorter events, 6.8 us)
Async XLA Ops:
  76.6 4.4 %copy-start.5 = (bf16[128,128]{1,0:T(8,128)(2,1)S(1)}, bf16[128,128]{1,0:T(8,128)(2,1)}, u32[]{:S(2)}) copy-start(bf16[128,128]{1,0:T(8,128)(2,1)} %param.4) | copy-start | bytes 98308
  76.6 11.5 %all-to-all-start.1 = ((bf16[256,8,128]{0,2,1:T(8,128)(2,1)}), bf16[256,8,128]{0,2,1:T(8,128)(2,1)S(1)}, u32[]{:S(2)}, u32[]{:S(2)}) async-start(bf16[256,8,128]{0,2,1:T(8,128)(2,1)} %bitcast.4), calls=%async_computation.1 | async-start | bytes 1048576 | tf_op jit(solution)/shard_map/all_to_all | solution.py:145
  80.9 0.8 copy-start.6
  88.1 11.8 %all-to-all-start.2 = ((bf16[256,8,128]{0,2,1:T(8,128)(2,1)}), bf16[256,8,128]{0,2,1:T(8,128)(2,1)S(1)}, u32[]{:S(2)}, u32[]{:S(2)}) async-start(bf16[256,8,128]{0,2,1:T(8,128)(2,1)} %bitcast.16), calls=%async_computation.2 | async-start | bytes 1048576 | tf_op jit(solution)/shard_map/all_to_all | solution.py:146
  102.3 1.1 copy-start.2
  147.3 1.0 copy-start.3
  189.9 0.8 copy-start
  209.4 66.6 %all-to-all-start.4 = ((f32[64,256,16]{1,2,0:T(8,128)}), f32[64,256,16]{1,2,0:T(8,128)}, u32[]{:S(2)}, u32[]{:S(2)}) async-start(f32[64,256,16]{1,2,0:T(8,128)} %bitcast.186), calls=%async_computation.4 | async-start | bytes 2097152 | tf_op jit(solution)/shard_map/all_to_all | solution.py:62
  220.3 1.0 copy-start.1
  221.4 1.0 copy-start.4
